TPU v7x, 32 devices: a whole 2x2x4 slice. The times are simulated.
32 devices in a mesh: wide: 8 (over z, x), narrow: 4 (over y, core).
Axes of the slice: x: 2, y: 2, z: 4, core: 2. Of those that a mesh axis runs over, the one named last changes fastest.
Arguments:
- activations: bfloat16 [2048, 16384], P('wide', 'narrow'), may hold values from -6 to 6
- grad_out: bfloat16 [2048, 8192], P('narrow', 'wide'), may hold values from -0.125 to 0.125
- momentum: float32 [8192, 16384], P('wide', 'narrow'), may hold values from -90 to 90
- right_factor: float32 [16384, 512], P('narrow'), may hold values from -0.046875 to 0.046875
Outputs:
- new_momentum: float32 [8192, 16384], P('wide', 'narrow')
- new_right: float32 [16384, 512], P('narrow')
- update: bfloat16 [8192, 16384], P('wide', 'narrow')
All inputs are finite; a program needn't handle non-finite values.
Results may differ from a plain program's by a relative error of at most 0.0012.
Values may be sent and summed in bfloat16 or wider, within the bound.
No kernel may reach another device: no remote copies, remote signals or barrier semaphores. Data moves between devices by JAX's collectives and lax.ppermute only.
A program may use at most 128 MiB of HBM per device.

v0:
```python
import math
import jax
import jax.numpy as jnp
from jax import lax
from jax.sharding import PartitionSpec as P

DOUT = 8192
DIN = 16384
RANK = 512
FEEDBACK = 0.05
EPSILON = 1e-06


def body(activations, grad_out, momentum, right_factor):
    highest = lax.Precision.HIGHEST
    out_rows = lax.all_gather(grad_out, "narrow", axis=0, tiled=True)
    gradient = lax.dot_general(
        out_rows,
        lax.all_gather(activations, "wide", axis=0, tiled=True),
        (((0,), (0,)), ((), ())),
        preferred_element_type=jnp.float32,
    )
    buffer = momentum + gradient
    partial_left = jnp.dot(
        buffer, right_factor, precision=highest, preferred_element_type=jnp.float32
    )
    left_factor = lax.psum(partial_left, "narrow")
    gram_local = jnp.dot(
        left_factor.T, left_factor, precision=highest, preferred_element_type=jnp.float32
    )
    gram_matrix = lax.psum(gram_local, "wide")
    lower_factor = jnp.linalg.cholesky(gram_matrix)
    ortho_left = jax.scipy.linalg.solve_triangular(lower_factor, left_factor.T, lower=True).T
    right_share = lax.psum_scatter(
        lax.dot_general(
            buffer,
            ortho_left,
            (((0,), (0,)), ((), ())),
            precision=highest,
            preferred_element_type=jnp.float32,
        ),
        "wide",
        scatter_dimension=0,
        tiled=True,
    )
    col_squares = lax.psum(jnp.sum(right_share * right_share, axis=0), ("wide", "narrow"))
    right_raw = lax.all_gather(right_share, "wide", axis=0, tiled=True)
    feedback = lax.dot_general(
        ortho_left,
        right_raw,
        (((1,), (1,)), ((), ())),
        precision=highest,
        preferred_element_type=jnp.float32,
    )
    new_momentum = buffer - FEEDBACK * feedback
    new_right = right_raw / (jnp.sqrt(col_squares) + EPSILON)
    update_scale = math.sqrt(DOUT * DIN / RANK)
    product = lax.dot_general(
        ortho_left,
        new_right,
        (((1,), (1,)), ((), ())),
        precision=highest,
        preferred_element_type=jnp.float32,
    )
    update = (update_scale * product).astype(jnp.bfloat16)
    return (new_momentum, new_right, update)


def solution(mesh):
    return jax.shard_map(
        body,
        mesh=mesh,
        in_specs=(P("wide", "narrow"), P("narrow", "wide"), P("wide", "narrow"), P("narrow", None)),
        out_specs=(P("wide", "narrow"), P("narrow", None), P("wide", "narrow")),
        check_vma=False,
    )
```

profile of v0, /device:TPU:0, one launch (start us, length us, event | category | flops | bytes accessed | tf_op | source)
XLA Modules:
  0.0 1089.3 jit_solution(18141778755275494876)
XLA Ops:
  7.2 0.7 all-gather.4.cloned.1.call-update
  7.9 0.7 all-gather.6.cloned.1.call-update
  8.6 0.0 all-reduce.4.cloned.1.call-start
  8.7 38.1 %all-gather.4.cloned.1.call-done = bf16[2048,1024]{1,0:T(8,128)(2,1)} async-done(((bf16[512,1024]{1,0:T(8,128)(2,1)}), bf16[2048,1024]{1,0:T(8,128)(2,1)}) %all-gather.4.cloned.1.call-update) | async-done | bytes 4194320 | tf_op jit(solution)/shard_map/all_gather | solution.py:16
  46.7 229.4 %all-gather.6.cloned.1.call-done = bf16[2048,4096]{1,0:T(8,128)(2,1)} async-done(((bf16[256,4096]{1,0:T(8,128)(2,1)}), bf16[2048,4096]{1,0:T(8,128)(2,1)}) %all-gather.6.cloned.1.call-update) | async-done | bytes 16777232 | tf_op jit(solution)/shard_map/all_gather | solution.py:19
  276.2 28.3 %convolution_add_fusion = f32[1024,4096]{1,0:T(8,128)} fusion(f32[1024,4096]{1,0:T(8,128)} %param.6, bf16[2048,1024]{1,0:T(8,128)(2,1)} %all-gather.4.cloned.1.call-done, bf16[2048,4096]{1,0:T(8,128)(2,1)} %all-gather.6.cloned.1.call-done), kind=kOutput, calls=%fused_computation.4 | convolution fusion | flops 17184063488 | bytes 54525952 | tf_op jit(solution)/shard_map/dot_general | solution.py:17
  304.5 31.4 %fusion.39 = f32[1024,512]{1,0:T(8,128)} fusion(f32[1024,4096]{1,0:T(8,128)} %convolution_add_fusion, f32[4096,512]{1,0:T(8,128)} %param.7), kind=kOutput, calls=%fused_computation.78 | convolution fusion | flops 25769803776 | bytes 27262976 | tf_op jit(solution)/shard_map/dot_general | solution.py:24
  335.9 0.0 all-reduce.6.cloned.1.call-start
  336.0 49.7 %all-reduce.4.cloned.1.call-done = f32[1024,512]{1,0:T(8,128)} async-done(((f32[1024,512]{1,0:T(8,128)}), f32[1024,512]{1,0:T(8,128)}) %all-reduce.4.cloned.1.call-update) | async-done | bytes 2097168 | tf_op jit(solution)/shard_map/psum | solution.py:27
  385.6 6.7 fusion.40
  392.4 0.2 reduce-scatter.2.cloned.1.call-start
  392.6 78.3 %all-reduce.6.cloned.1.call-done = f32[512,512]{0,1:T(8,128)} async-done(((f32[512,512]{0,1:T(8,128)}), f32[512,512]{0,1:T(8,128)}) %all-reduce.6.cloned.1.call-update) | async-done | bytes 1048592 | tf_op jit(solution)/shard_map/psum | solution.py:31
  470.9 1.6 copy.8
  472.5 1.4 fusion.12
  473.9 1.0 copy-done.3
  474.9 11.7 %cholesky.104 = f32[128,128]{1,0:T(8,128)S(1)} custom-call(f32[128,128]{1,0:T(8,128)S(1)} %cholesky.266), custom_call_target="Cholesky" | custom-call | tf_op jit(solution)/shard_map/jit(cholesky)/cholesky | solution.py:32
  486.7 0.1 cholesky.224
  486.8 9.8 custom-call.31
  496.6 1.2 constant_dynamic-update-slice_fusion.3
  497.8 1.3 convolution_subtract_fusion.2
  499.1 11.7 %cholesky.217 = f32[128,128]{1,0:T(8,128)S(1)} custom-call(f32[128,128]{1,0:T(8,128)S(1)} %cholesky.270), custom_call_target="Cholesky" | custom-call | tf_op jit(solution)/shard_map/jit(cholesky)/cholesky | solution.py:32
  510.9 10.0 custom-call.32
  520.9 0.3 convolution_dynamic-update-slice_fusion
  521.1 1.3 convolution_subtract_fusion.3
  522.5 11.7 %cholesky.238 = f32[128,128]{1,0:T(8,128)S(1)} custom-call(f32[128,128]{1,0:T(8,128)S(1)} %cholesky.275), custom_call_target="Cholesky" | custom-call | tf_op jit(solution)/shard_map/jit(cholesky)/cholesky | solution.py:32
  534.2 9.8 custom-call.33
  544.0 0.2 convolution_dynamic-update-slice_fusion.1
  544.2 1.2 convolution_subtract_fusion.4
  545.5 11.7 %cholesky.255 = f32[128,128]{1,0:T(8,128)S(1)} custom-call(f32[128,128]{1,0:T(8,128)S(1)} %convolution_subtract_fusion.4), custom_call_target="Cholesky" | custom-call | tf_op jit(solution)/shard_map/jit(cholesky)/cholesky | solution.py:32
  557.2 0.7 compare_reduce_fusion.1
  557.9 0.6 compare_reduce_fusion
  558.5 0.7 compare_reduce_fusion.2
  561.7 1.6 select_select_fusion
  563.3 13.6 %while.1 = (s32[]{:T(128)}, f32[512,512]{1,0:T(8,128)}, s32[4,2]{0,1:T(2,128)S(1)}, f32[4,128,128]{2,1,0:T(8,128)}, s32[]{:T(128)}) while((s32[]{:T(128)}, f32[512,512]{1,0:T(8,128)}, s32[4,2]{0,1:T(2,128)S(1)}, f32[4,128,128]{2,1,0:T(8,128)}, s32[]{:T(128)}) %tuple.31), condition=%wide.while_cond, body=%wide.while_body.sunk | while | flops 2 | bytes 132205 | solution.py:33
  563.3 0.1 constant_dynamic-slice_fusion.2
  563.3 0.5 fusion.56
  563.9 2.8 bitcast_dynamic-update-slice_fusion.2
  566.7 0.1 constant_dynamic-slice_fusion.2
  566.8 0.5 fusion.56
  567.3 2.8 bitcast_dynamic-update-slice_fusion.2
  570.1 0.1 constant_dynamic-slice_fusion.2
  570.2 0.5 fusion.56
  570.7 2.8 bitcast_dynamic-update-slice_fusion.2
  573.5 0.1 constant_dynamic-slice_fusion.2
  573.6 0.5 fusion.56
  574.1 2.8 bitcast_dynamic-update-slice_fusion.2
  576.9 40.1 %custom-call.34 = f32[4,128,128]{1,2,0:T(8,128)S(1)} custom-call(f32[4,128,128]{2,1,0:T(8,128)} %get-tuple-element.10), custom_call_target="InvertDiagBlocksLowerTriangular" | custom-call | tf_op jit(solution)/shard_map/jit(_solve_triangular)/triangular_solve | solution.py:33
  617.0 0.6 fusion.13
  617.7 1.8 convolution_subtract_fusion.1
  619.5 0.6 fusion.27
  620.2 2.9 convolution_subtract_fusion
  623.0 0.6 fusion.25
  623.7 3.8 fusion.6
  627.5 0.6 fusion.24
  628.2 0.8 copy-done.4
  629.0 56.3 %fusion.15 = f32[4096,512]{1,0:T(8,128)} fusion(f32[1024,4096]{1,0:T(8,128)} %convolution_add_fusion, f32[128,1024]{1,0:T(8,128)S(1)} %fusion.24, f32[128,1024]{1,0:T(8,128)S(1)} %fusion.25, f32[128,1024]{1,0:T(8,128)S(1)} %fusion.27, f32[128,1024]{1,0:T(8,128)S(1)} %fusion.13), kind=kOutput, calls=%fused_computation.31 | convolution fusion | flops 25771376640 | bytes 27262976 | tf_op jit(solution)/shard_map/dot_general | solution.py:35
  685.3 0.0 all-gather.8.cloned.1.call-start
  685.4 147.2 %reduce-scatter.2.cloned.1.call-done = f32[512,512]{1,0:T(8,128)} async-done(((f32[4096,512]{1,0:T(8,128)}), f32[512,512]{1,0:T(8,128)}) %reduce-scatter.2.cloned.1.call-update) | async-done | bytes 1048592 | tf_op jit(solution)/shard_map/reduce_scatter | solution.py:34
  832.6 1.3 multiply_reduce_fusion
  833.9 43.3 %psum.23 = f32[512]{0:T(512)S(1)} all-reduce(f32[512]{0:T(512)S(1)} %multiply_reduce_fusion), channel_id=1, replica_groups=mesh['wide'=8,'narrow'=4] {'wide','narrow'}, use_global_device_ids=true, to_apply=%region_12.13 | all-reduce | flops 512 | bytes 4096 | tf_op jit(solution)/shard_map/psum | solution.py:46
  877.2 82.0 %all-gather.8.cloned.1.call-done = f32[4096,512]{1,0:T(8,128)} async-done(((f32[512,512]{1,0:T(8,128)}), f32[4096,512]{1,0:T(8,128)}) %all-gather.8.cloned.1.call-update) | async-done | bytes 8388624 | tf_op jit(solution)/shard_map/all_gather | solution.py:47
  959.2 8.9 broadcast_divide_fusion
  968.1 56.8 %multiply_convert_fusion = bf16[1024,4096]{1,0:T(8,128)(2,1)} fusion(f32[4096,512]{1,0:T(8,128)} %broadcast_divide_fusion, f32[128,1024]{1,0:T(8,128)} %copy-done.4, f32[128,1024]{1,0:T(8,128)} %copy-done.2, f32[128,1024]{1,0:T(8,128)} %copy-done.1, f32[128,1024]{1,0:T(8,128)S(1)} %fusion.13), kind=kOutput, calls=%fused_computation.2 | convolution fusion | flops 25779765248 | bytes 18874368 | tf_op jit(solution)/shard_map/dot_general | solution.py:58
  1025.0 57.3 %multiply_subtract_fusion = f32[1024,4096]{1,0:T(8,128)} fusion(f32[1024,4096]{1,0:T(8,128)S(1)} %bitcast.65, f32[4096,512]{1,0:T(8,128)S(1)} %bitcast.59, f32[128,1024]{1,0:T(8,128)} %copy-done.4, f32[128,1024]{1,0:T(8,128)} %copy-done.2, f32[128,1024]{1,0:T(8,128)} %copy-done.1, f32[128,1024]{1,0:T(8,128)S(1)} %fusion.13), kind=kOutput, calls=%fused_computation.3 | convolution fusion | flops 25779765248 | bytes 44040192 | tf_op jit(solution)/shard_map/dot_general | solution.py:48
  (39 shorter events, 0.4 us)
Async XLA Ops:
  7.2 39.6 %all-gather.4.cloned.1.call-start = ((), (), s32[]{:S(2)}) async-start(), calls=%async_computation.1 | async-start | bytes 5242880 | tf_op jit(solution)/shard_map/all_gather | solution.py:16
  7.9 268.3 %all-gather.6.cloned.1.call-start = ((), (), s32[]{:S(2)}) async-start(), calls=%async_computation.2 | async-start | bytes 18874368 | tf_op jit(solution)/shard_map/all_gather | solution.py:19
  8.6 377.0 %all-reduce.4.cloned.1.call-start = ((), (), s32[]{:S(2)}) async-start(), calls=%async_computation.3 | async-start | bytes 4194304 | tf_op jit(solution)/shard_map/psum | solution.py:27
  335.9 135.0 %all-reduce.6.cloned.1.call-start = ((), (), s32[]{:S(2)}) async-start(), calls=%async_computation.4 | async-start | bytes 2097152 | tf_op jit(solution)/shard_map/psum | solution.py:31
  392.4 440.2 %reduce-scatter.2.cloned.1.call-start = ((), (), s32[]{:S(2)}) async-start(), calls=%async_computation.5 | async-start | bytes 9437184 | tf_op jit(solution)/shard_map/reduce_scatter | solution.py:34
  473.9 1.0 copy-start.3
  474.9 142.1 %copy-start = (f32[1024,512]{1,0:T(8,128)S(1)}, f32[1024,512]{1,0:T(8,128)}, u32[]{:S(2)}) copy-start(f32[1024,512]{1,0:T(8,128)} %all-reduce.4.cloned.1.call-done) | copy-start | bytes 6291460
  620.2 65.1 %copy-start.1 = (f32[128,1024]{1,0:T(8,128)}, f32[128,1024]{1,0:T(8,128)S(1)}, u32[]{:S(2)}) copy-start(f32[128,1024]{1,0:T(8,128)S(1)} %fusion.27) | copy-start | bytes 1572868
  623.7 4.5 copy-start.2
  628.2 0.8 copy-start.4
  685.3 273.9 %all-gather.8.cloned.1.call-start = ((), (), s32[]{:S(2)}) async-start(), calls=%async_computation.6 | async-start | bytes 9437184 | tf_op jit(solution)/shard_map/all_gather | solution.py:47
  959.2 65.7 %slice-start = ((s8[8388608]{0:T(1024)(128)(4,1)}), s8[4194304]{0:T(1024)(128)(4,1)S(1)}, s32[]{:S(2)}) async-start(s8[8388608]{0:T(1024)(128)(4,1)} %bitcast.58), calls=%async_computation.7 | async-start | bytes 8388608
  959.2 65.7 %slice-start.2 = ((s8[16777216]{0:T(1024)(128)(4,1)}), s8[4194304]{0:T(1024)(128)(4,1)S(1)}, s32[]{:S(2)}) async-start(s8[16777216]{0:T(1024)(128)(4,1)} %bitcast.64), calls=%async_computation.9 | async-start | bytes 8388608
  959.2 65.7 %slice-start.3 = ((s8[16777216]{0:T(1024)(128)(4,1)}), s8[4194304]{0:T(1024)(128)(4,1)S(1)}, s32[]{:S(2)}) async-start(s8[16777216]{0:T(1024)(128)(4,1)} %bitcast.64), calls=%async_computation.10 | async-start | bytes 8388608
  968.1 56.8 %slice-start.1 = ((s8[8388608]{0:T(1024)(128)(4,1)}), s8[4194304]{0:T(1024)(128)(4,1)S(1)}, s32[]{:S(2)}) async-start(s8[8388608]{0:T(1024)(128)(4,1)} %bitcast.58), calls=%async_computation.8 | async-start | bytes 8388608
  968.1 56.8 %slice-start.4 = ((s8[16777216]{0:T(1024)(128)(4,1)}), s8[4194304]{0:T(1024)(128)(4,1)S(1)}, s32[]{:S(2)}) async-start(s8[16777216]{0:T(1024)(128)(4,1)} %bitcast.64), calls=%async_computation.11 | async-start | bytes 8388608
  968.1 56.8 %slice-start.5 = ((s8[16777216]{0:T(1024)(128)(4,1)}), s8[4194304]{0:T(1024)(128)(4,1)S(1)}, s32[]{:S(2)}) async-start(s8[16777216]{0:T(1024)(128)(4,1)} %bitcast.64), calls=%async_computation.12 | async-start | bytes 8388608
Sparse Core Ops, SparseCore 0:
  9.5 37.1 all-gather.3
  48.9 227.2 all-gather.5
  336.0 49.5 all-reduce.3
  392.5 78.3 all-reduce.5
  685.4 147.0 reduce-scatter.1
  834.5 124.6 all-gather.7
where the time goes:
time: 1100 us; the launch traced here: 1090 us
  waiting for transfers between devices  626 us (57%)
  matrix products  253 us (23%)
  other arithmetic  132 us (12%)
  blocking collectives  43.3 us (4%)
  local copies, waits for them, and re-layouts  17.1 us (2%)
  between operations  17.1 us (2%)
    all_gather x1, waiting for transfers between devices, body(): lax.all_gather(activations, 'wide', axis=0, tiled=True)  229 us
    reduce_scatter x1, waiting for transfers between devices, body(): lax.psum_scatter(lax.dot_general(buffer, ortho_left, (((0,), (0,)), ((),...  147 us
    all_gather x1, waiting for transfers between devices, body(): right_raw = lax.all_gather(right_share, 'wide', axis=0, tiled=True)  82 us
    another operation x14, other arithmetic, body(): lower_factor = jnp.linalg.cholesky(gram_matrix)  78.6 us
    psum x1, waiting for transfers between devices, body(): gram_matrix = lax.psum(gram_local, 'wide')  78.3 us
    dot_general x1, matrix products, body(): lax.dot_general(ortho_left, right_raw, (((1,), (1,)), ((), ())), precisio...  57.3 us
    dot_general x1, matrix products, body(): lax.dot_general(ortho_left, new_right, (((1,), (1,)), ((), ())), precisio...  56.8 us
    dot_general x1, matrix products, body(): lax.dot_general(buffer, ortho_left, (((0,), (0,)), ((), ())), precision=h...  56.3 us
  transfers between devices with their start and end apart: 6, of which 6 were waited for; matrix products, arithmetic and copies ran while one was open for 0% of the time, Pallas kernels for 0%

commit v1 on v0

--- a/solution.py
+++ b/solution.py
@@ -9,6 +9,11 @@
 RANK = 512
 FEEDBACK = 0.05
 EPSILON = 1e-06
+
+
+def summed_here(array, name):
+    parts = lax.all_gather(array, name)
+    return jnp.sum(parts, axis=0)
 
 
 def body(activations, grad_out, momentum, right_factor):
@@ -28,7 +33,7 @@
     gram_local = jnp.dot(
         left_factor.T, left_factor, precision=highest, preferred_element_type=jnp.float32
     )
-    gram_matrix = lax.psum(gram_local, "wide")
+    gram_matrix = summed_here(gram_local, "wide")
     lower_factor = jnp.linalg.cholesky(gram_matrix)
     ortho_left = jax.scipy.linalg.solve_triangular(lower_factor, left_factor.T, lower=True).T
     right_share = lax.psum_scatter(

time: 1100 us -> 1140 us (1.036)
  waiting for transfers between devices: 626 us -> 671 us
    all_gather x0 -> x1, waiting for transfers between devices: none -> 124 us  [summed_here(): parts = lax.all_gather(array, name)]
    psum x1 -> x0, waiting for transfers between devices: 78.3 us -> none  [body(): gram_matrix = lax.psum(gram_local, 'wide')]
where the time goes in v1:
time: 1140 us
  waiting for transfers between devices  671 us (59%)
  matrix products  253 us (22%)
  other arithmetic  135 us (12%)
  blocking collectives  43.3 us (4%)
  between operations  17.1 us (2%)
  local copies, waits for them, and re-layouts  15.8 us (1%)
    all_gather x1, waiting for transfers between devices, body(): lax.all_gather(activations, 'wide', axis=0, tiled=True)  229 us
    reduce_scatter x1, waiting for transfers between devices, body(): lax.psum_scatter(lax.dot_general(buffer, ortho_left, (((0,), (0,)), ((),...  146 us
    all_gather x1, waiting for transfers between devices, summed_here(): parts = lax.all_gather(array, name)  124 us
    all_gather x1, waiting for transfers between devices, body(): right_raw = lax.all_gather(right_share, 'wide', axis=0, tiled=True)  82 us
    another operation x14, other arithmetic, body(): lower_factor = jnp.linalg.cholesky(gram_matrix)  79.1 us
    dot_general x1, matrix products, body(): lax.dot_general(ortho_left, right_raw, (((1,), (1,)), ((), ())), precisio...  57.3 us
    dot_general x1, matrix products, body(): lax.dot_general(ortho_left, new_right, (((1,), (1,)), ((), ())), precisio...  56.8 us
    dot_general x1, matrix products, body(): lax.dot_general(buffer, ortho_left, (((0,), (0,)), ((), ())), precision=h...  56.3 us
  transfers between devices with their start and end apart: 6, of which 6 were waited for; matrix products, arithmetic and copies ran while one was open for 0% of the time, Pallas kernels for 0%

profile of v1, /device:TPU:0, one launch (start us, length us, event | category | flops | bytes accessed | tf_op | source)
XLA Modules:
  0.0 1136.0 jit_solution(14320133369232768248)
XLA Ops:
  7.2 0.7 all-gather.6.cloned.1.call-update
  7.9 0.7 all-gather.8.cloned.1.call-update
  8.7 38.1 %all-gather.6.cloned.1.call-done = bf16[2048,1024]{1,0:T(8,128)(2,1)} async-done(((bf16[512,1024]{1,0:T(8,128)(2,1)}), bf16[2048,1024]{1,0:T(8,128)(2,1)}) %all-gather.6.cloned.1.call-update) | async-done | bytes 4194320 | tf_op jit(solution)/shard_map/all_gather | solution.py:21
  46.7 229.4 %all-gather.8.cloned.1.call-done = bf16[2048,4096]{1,0:T(8,128)(2,1)} async-done(((bf16[256,4096]{1,0:T(8,128)(2,1)}), bf16[2048,4096]{1,0:T(8,128)(2,1)}) %all-gather.8.cloned.1.call-update) | async-done | bytes 16777232 | tf_op jit(solution)/shard_map/all_gather | solution.py:24
  276.2 28.3 %convolution_add_fusion = f32[1024,4096]{1,0:T(8,128)} fusion(f32[1024,4096]{1,0:T(8,128)} %param.6, bf16[2048,1024]{1,0:T(8,128)(2,1)} %all-gather.6.cloned.1.call-done, bf16[2048,4096]{1,0:T(8,128)(2,1)} %all-gather.8.cloned.1.call-done), kind=kOutput, calls=%fused_computation.4 | convolution fusion | flops 17184063488 | bytes 54525952 | tf_op jit(solution)/shard_map/dot_general | solution.py:22
  304.5 31.4 %fusion.39 = f32[1024,512]{1,0:T(8,128)} fusion(f32[1024,4096]{1,0:T(8,128)} %convolution_add_fusion, f32[4096,512]{1,0:T(8,128)} %param.7), kind=kOutput, calls=%fused_computation.78 | convolution fusion | flops 25769803776 | bytes 27262976 | tf_op jit(solution)/shard_map/dot_general | solution.py:29
  335.9 0.0 all-gather.12.cloned.1.call-start
  336.0 49.7 %all-reduce.3.cloned.1.call-done = f32[1024,512]{1,0:T(8,128)} async-done(((f32[1024,512]{1,0:T(8,128)}), f32[1024,512]{1,0:T(8,128)}) %all-reduce.3.cloned.1.call-update) | async-done | bytes 2097168 | tf_op jit(solution)/shard_map/psum | solution.py:32
  385.6 6.7 fusion.40
  392.3 0.2 reduce-scatter.2.cloned.1.call-start
  392.6 124.4 %all-gather.12.cloned.1.call-done = f32[4096,512]{1,0:T(8,128)} async-done(((f32[512,512]{1,0:T(8,128)}), f32[4096,512]{1,0:T(8,128)}) %all-gather.12.cloned.1.call-update) | async-done | bytes 8388624 | tf_op jit(solution)/shard_map/all_gather | solution.py:15
  517.0 4.5 reduce_sum.18
  521.5 0.3 copy.8
  521.8 0.2 fusion.12
  522.1 1.0 copy-done.3
  523.1 11.7 %cholesky.104 = f32[128,128]{1,0:T(8,128)S(1)} custom-call(f32[128,128]{1,0:T(8,128)S(1)} %cholesky.266), custom_call_target="Cholesky" | custom-call | tf_op jit(solution)/shard_map/jit(cholesky)/cholesky | solution.py:37
  534.8 0.1 cholesky.224
  534.9 9.8 custom-call.31
  544.8 1.2 constant_dynamic-update-slice_fusion.3
  546.0 1.3 convolution_subtract_fusion.2
  547.3 11.9 %cholesky.217 = f32[128,128]{1,0:T(8,128)S(1)} custom-call(f32[128,128]{1,0:T(8,128)S(1)} %cholesky.270), custom_call_target="Cholesky" | custom-call | tf_op jit(solution)/shard_map/jit(cholesky)/cholesky | solution.py:37
  559.2 9.8 custom-call.32
  569.0 0.3 convolution_dynamic-update-slice_fusion
  569.3 1.3 convolution_subtract_fusion.3
  570.6 11.7 %cholesky.238 = f32[128,128]{1,0:T(8,128)S(1)} custom-call(f32[128,128]{1,0:T(8,128)S(1)} %cholesky.275), custom_call_target="Cholesky" | custom-call | tf_op jit(solution)/shard_map/jit(cholesky)/cholesky | solution.py:37
  582.4 9.8 custom-call.33
  592.2 0.2 convolution_dynamic-update-slice_fusion.1
  592.4 1.2 convolution_subtract_fusion.4
  593.6 12.2 %cholesky.255 = f32[128,128]{1,0:T(8,128)S(1)} custom-call(f32[128,128]{1,0:T(8,128)S(1)} %convolution_subtract_fusion.4), custom_call_target="Cholesky" | custom-call | tf_op jit(solution)/shard_map/jit(cholesky)/cholesky | solution.py:37
  605.8 0.6 compare_reduce_fusion.1
  606.5 0.6 compare_reduce_fusion
  607.1 0.7 compare_reduce_fusion.2
  610.3 1.1 select_select_fusion
  611.4 13.6 %while.1 = (s32[]{:T(128)}, f32[512,512]{1,0:T(8,128)}, s32[4,2]{0,1:T(2,128)S(1)}, f32[4,128,128]{2,1,0:T(8,128)}, s32[]{:T(128)}) while((s32[]{:T(128)}, f32[512,512]{1,0:T(8,128)}, s32[4,2]{0,1:T(2,128)S(1)}, f32[4,128,128]{2,1,0:T(8,128)}, s32[]{:T(128)}) %tuple.31), condition=%wide.while_cond, body=%wide.while_body.sunk | while | flops 2 | bytes 132205 | solution.py:38
  611.4 0.1 constant_dynamic-slice_fusion.2
  611.5 0.5 fusion.56
  612.0 2.8 bitcast_dynamic-update-slice_fusion.2
  614.9 0.1 constant_dynamic-slice_fusion.2
  614.9 0.5 fusion.56
  615.5 2.8 bitcast_dynamic-update-slice_fusion.2
  618.3 0.1 constant_dynamic-slice_fusion.2
  618.3 0.5 fusion.56
  618.9 2.8 bitcast_dynamic-update-slice_fusion.2
  621.7 0.1 constant_dynamic-slice_fusion.2
  621.7 0.5 fusion.56
  622.3 2.7 bitcast_dynamic-update-slice_fusion.2
  625.0 40.1 %custom-call.34 = f32[4,128,128]{1,2,0:T(8,128)S(1)} custom-call(f32[4,128,128]{2,1,0:T(8,128)} %get-tuple-element.10), custom_call_target="InvertDiagBlocksLowerTriangular" | custom-call | tf_op jit(solution)/shard_map/jit(_solve_triangular)/triangular_solve | solution.py:38
  665.2 0.6 fusion.13
  665.8 1.8 convolution_subtract_fusion.1
  667.7 0.6 fusion.27
  668.3 2.9 convolution_subtract_fusion
  671.2 0.6 fusion.25
  671.8 3.8 fusion.6
  675.7 0.6 fusion.24
  676.3 0.8 copy-done.4
  677.1 56.3 %fusion.15 = f32[4096,512]{1,0:T(8,128)} fusion(f32[1024,4096]{1,0:T(8,128)} %convolution_add_fusion, f32[128,1024]{1,0:T(8,128)S(1)} %fusion.24, f32[128,1024]{1,0:T(8,128)S(1)} %fusion.25, f32[128,1024]{1,0:T(8,128)S(1)} %fusion.27, f32[128,1024]{1,0:T(8,128)S(1)} %fusion.13), kind=kOutput, calls=%fused_computation.31 | convolution fusion | flops 25771376640 | bytes 27262976 | tf_op jit(solution)/shard_map/dot_general | solution.py:40
  733.4 0.0 all-gather.10.cloned.1.call-start
  733.5 145.7 %reduce-scatter.2.cloned.1.call-done = f32[512,512]{1,0:T(8,128)} async-done(((f32[4096,512]{1,0:T(8,128)}), f32[512,512]{1,0:T(8,128)}) %reduce-scatter.2.cloned.1.call-update) | async-done | bytes 1048592 | tf_op jit(solution)/shard_map/reduce_scatter | solution.py:39
  879.3 1.3 multiply_reduce_fusion
  880.6 43.3 %psum.15 = f32[512]{0:T(512)S(1)} all-reduce(f32[512]{0:T(512)S(1)} %multiply_reduce_fusion), channel_id=1, replica_groups=mesh['wide'=8,'narrow'=4] {'wide','narrow'}, use_global_device_ids=true, to_apply=%region_12.13 | all-reduce | flops 512 | bytes 4096 | tf_op jit(solution)/shard_map/psum | solution.py:51
  923.9 82.0 %all-gather.10.cloned.1.call-done = f32[4096,512]{1,0:T(8,128)} async-done(((f32[512,512]{1,0:T(8,128)}), f32[4096,512]{1,0:T(8,128)}) %all-gather.10.cloned.1.call-update) | async-done | bytes 8388624 | tf_op jit(solution)/shard_map/all_gather | solution.py:52
  1005.9 8.9 broadcast_divide_fusion
  1014.8 56.8 %multiply_convert_fusion = bf16[1024,4096]{1,0:T(8,128)(2,1)} fusion(f32[4096,512]{1,0:T(8,128)} %broadcast_divide_fusion, f32[128,1024]{1,0:T(8,128)} %copy-done.4, f32[128,1024]{1,0:T(8,128)} %copy-done.2, f32[128,1024]{1,0:T(8,128)} %copy-done.1, f32[128,1024]{1,0:T(8,128)S(1)} %fusion.13), kind=kOutput, calls=%fused_computation.2 | convolution fusion | flops 25779765248 | bytes 18874368 | tf_op jit(solution)/shard_map/dot_general | solution.py:63
  1071.7 57.3 %multiply_subtract_fusion = f32[1024,4096]{1,0:T(8,128)} fusion(f32[1024,4096]{1,0:T(8,128)S(1)} %bitcast.66, f32[4096,512]{1,0:T(8,128)S(1)} %bitcast.60, f32[128,1024]{1,0:T(8,128)} %copy-done.4, f32[128,1024]{1,0:T(8,128)} %copy-done.2, f32[128,1024]{1,0:T(8,128)} %copy-done.1, f32[128,1024]{1,0:T(8,128)S(1)} %fusion.13), kind=kOutput, calls=%fused_computation.3 | convolution fusion | flops 25779765248 | bytes 44040192 | tf_op jit(solution)/shard_map/dot_general | solution.py:53
  (40 shorter events, 0.4 us)
Async XLA Ops:
  7.2 39.6 %all-gather.6.cloned.1.call-start = ((), (), s32[]{:S(2)}) async-start(), calls=%async_computation.1 | async-start | bytes 5242880 | tf_op jit(solution)/shard_map/all_gather | solution.py:21
  7.9 268.3 %all-gather.8.cloned.1.call-start = ((), (), s32[]{:S(2)}) async-start(), calls=%async_computation.2 | async-start | bytes 18874368 | tf_op jit(solution)/shard_map/all_gather | solution.py:24
  8.6 377.0 %all-reduce.3.cloned.1.call-start = ((), (), s32[]{:S(2)}) async-start(), calls=%async_computation.3 | async-start | bytes 4194304 | tf_op jit(solution)/shard_map/psum | solution.py:32
  335.9 181.1 %all-gather.12.cloned.1.call-start = ((), (), s32[]{:S(2)}) async-start(), calls=%async_computation.6 | async-start | bytes 9437184 | tf_op jit(solution)/shard_map/all_gather | solution.py:15
  392.3 486.9 %reduce-scatter.2.cloned.1.call-start = ((), (), s32[]{:S(2)}) async-start(), calls=%async_computation.4 | async-start | bytes 9437184 | tf_op jit(solution)/shard_map/reduce_scatter | solution.py:39
  522.1 1.0 copy-start.3
  523.0 142.1 %copy-start = (f32[1024,512]{1,0:T(8,128)S(1)}, f32[1024,512]{1,0:T(8,128)}, u32[]{:S(2)}) copy-start(f32[1024,512]{1,0:T(8,128)} %all-reduce.3.cloned.1.call-done) | copy-start | bytes 6291460
  668.3 65.1 %copy-start.1 = (f32[128,1024]{1,0:T(8,128)}, f32[128,1024]{1,0:T(8,128)S(1)}, u32[]{:S(2)}) copy-start(f32[128,1024]{1,0:T(8,128)S(1)} %fusion.27) | copy-start | bytes 1572868
  671.8 4.5 copy-start.2
  676.3 0.8 copy-start.4
  733.4 272.4 %all-gather.10.cloned.1.call-start = ((), (), s32[]{:S(2)}) async-start(), calls=%async_computation.5 | async-start | bytes 9437184 | tf_op jit(solution)/shard_map/all_gather | solution.py:52
  1005.9 65.7 %slice-start = ((s8[8388608]{0:T(1024)(128)(4,1)}), s8[4194304]{0:T(1024)(128)(4,1)S(1)}, s32[]{:S(2)}) async-start(s8[8388608]{0:T(1024)(128)(4,1)} %bitcast.59), calls=%async_computation.7 | async-start | bytes 8388608
  1005.9 65.7 %slice-start.2 = ((s8[16777216]{0:T(1024)(128)(4,1)}), s8[4194304]{0:T(1024)(128)(4,1)S(1)}, s32[]{:S(2)}) async-start(s8[16777216]{0:T(1024)(128)(4,1)} %bitcast.65), calls=%async_computation.9 | async-start | bytes 8388608
  1005.9 65.7 %slice-start.3 = ((s8[16777216]{0:T(1024)(128)(4,1)}), s8[4194304]{0:T(1024)(128)(4,1)S(1)}, s32[]{:S(2)}) async-start(s8[16777216]{0:T(1024)(128)(4,1)} %bitcast.65), calls=%async_computation.10 | async-start | bytes 8388608
  1014.8 56.8 %slice-start.1 = ((s8[8388608]{0:T(1024)(128)(4,1)}), s8[4194304]{0:T(1024)(128)(4,1)S(1)}, s32[]{:S(2)}) async-start(s8[8388608]{0:T(1024)(128)(4,1)} %bitcast.59), calls=%async_computation.8 | async-start | bytes 8388608
  1014.8 56.8 %slice-start.4 = ((s8[16777216]{0:T(1024)(128)(4,1)}), s8[4194304]{0:T(1024)(128)(4,1)S(1)}, s32[]{:S(2)}) async-start(s8[16777216]{0:T(1024)(128)(4,1)} %bitcast.65), calls=%async_computation.11 | async-start | bytes 8388608
  1014.8 56.8 %slice-start.5 = ((s8[16777216]{0:T(1024)(128)(4,1)}), s8[4194304]{0:T(1024)(128)(4,1)S(1)}, s32[]{:S(2)}) async-start(s8[16777216]{0:T(1024)(128)(4,1)} %bitcast.65), calls=%async_computation.12 | async-start | bytes 8388608
Sparse Core Ops, SparseCore 0:
  9.5 37.1 all-gather.5
  48.9 227.2 all-gather.7
  336.0 49.5 all-reduce.2
  392.4 124.5 all-gather.11
  733.6 145.6 reduce-scatter.1
  881.2 124.6 all-gather.9
